TPU v7x, 1024 devices: a whole 8x8x8 slice. The times are simulated.
1024 devices in a mesh: gx: 4 (over x_hi), gy: 16 (over x_lo, z), gz: 16 (over y, core).
Axes of the slice: x: 8 (x_hi: 4, x_lo: 2; x = x_hi * 2 + x_lo), y: 8, z: 8, core: 2. Of those that a mesh axis runs over, the one named last changes fastest.
Arguments:
- offsets: float32 [3, 8, 64, 16, 256], P(None, 'gx', 'gy', 'gz'), may hold values from 0 to 1
- velocity: float32 [3, 8, 64, 16, 256], P(None, 'gx', 'gy', 'gz'), may hold values from -6 to 6
- mass: float32 [8, 64, 16, 256], P('gx', 'gy', 'gz'), may hold values from 0.004 to 0.04
- counts: int32 [8, 64, 16], P('gx', 'gy', 'gz'), may hold values from 64 to 256
Outputs:
- new_offsets: float32 [3, 8, 64, 16, 256], P(None, 'gx', 'gy', 'gz')
- new_velocity: float32 [3, 8, 64, 16, 256], P(None, 'gx', 'gy', 'gz')
Inputs may be any that keep to these rules, and one draw needn't show every extreme that they name: `counts`: slots at or past a leaf's count are padding; their masses and positions carry no meaning as sources.
All inputs are finite; a program needn't handle non-finite values.
Results may differ from a plain program's by a relative error of at most 0.0001.
Values sent between devices are 32-bit elements; how exact they have to be, the bound alone decides.
A program may use at most 32 MiB of HBM per device.

v0:
```python
import jax
import jax.numpy as jnp
import numpy as np
from jax import lax
from jax.sharding import PartitionSpec as P

SUBSTEPS = 2


def with_halo(block, sides, width):
    for axis, dim in sides:
        count = lax.axis_size(axis)
        forward = [(i, i + 1) for i in range(count - 1)]
        forward.append((count - 1, 0))
        backward = [(target, source) for source, target in forward]
        low = lax.ppermute(
            lax.slice_in_dim(block, block.shape[dim] - width, None, axis=dim), axis, forward
        )
        high = lax.ppermute(lax.slice_in_dim(block, 0, width, axis=dim), axis, backward)
        block = jnp.concatenate([low, block, high], axis=dim)
    return block


def pair_tile(target, source_pos, source_mass, shift):
    dist = source_pos[..., None, :] - target[..., :, None]
    dist = dist + shift.reshape((3,) + (1,) * (dist.ndim - 1))
    square = jnp.sum(dist * dist, axis=0)
    factor = (square + 0.01) ** (-1.5) * jnp.maximum(1.0 - square, 0.0) ** 2
    scaled = source_mass[..., None, :] * factor
    return jnp.sum(scaled[None] * dist, axis=-1)


def ghosts(fields):
    return with_halo(fields, (("gx", 1), ("gy", 2), ("gz", 3)), 1)


def forces(position, padded_pos, padded_mass):
    span_x, span_y, span_z, slots = (
        position.shape[1],
        position.shape[2],
        position.shape[3],
        position.shape[4],
    )
    leaves = span_x * span_y * span_z
    block = 4
    blocks = leaves // block
    pos_list = []
    mass_list = []
    shift_list = []
    for step_a in (-1, 0, 1):
        for step_b in (-1, 0, 1):
            for step_c in (-1, 0, 1):
                lower = (1 + step_a, 1 + step_b, 1 + step_c)
                source_pos = padded_pos[
                    :,
                    lower[0] : lower[0] + span_x,
                    lower[1] : lower[1] + span_y,
                    lower[2] : lower[2] + span_z,
                    :,
                ]
                source_mass = padded_mass[
                    lower[0] : lower[0] + span_x,
                    lower[1] : lower[1] + span_y,
                    lower[2] : lower[2] + span_z,
                    :,
                ]
                pos_list.append(source_pos.reshape(3, blocks, block, slots))
                mass_list.append(source_mass.reshape(blocks, block, slots))
                shift_list.append([step_a, step_b, step_c])
    all_pos = jnp.moveaxis(jnp.stack(pos_list), 2, 0)
    all_mass = jnp.moveaxis(jnp.stack(mass_list), 1, 0)
    shifts = jnp.array(np.array(shift_list, dtype=np.float32))
    targets = jnp.moveaxis(position.reshape(3, blocks, block, slots), 1, 0)

    def one_block(items):
        target, source_pos, source_mass = items

        def one_offset(total, parts):
            return (total + pair_tile(target, parts[0], parts[1], parts[2]), None)

        total, _ = lax.scan(one_offset, jnp.zeros_like(target), (source_pos, source_mass, shifts))
        return total

    result = lax.map(one_block, (targets, all_pos, all_mass))
    return jnp.moveaxis(result, 0, 1).reshape(position.shape)


def shards(offsets, velocity, mass, counts):
    slot = jnp.arange(mass.shape[-1], dtype=jnp.int32)
    weight = jnp.where(slot < counts[..., None], mass, jnp.float32(0.0))
    position, speed = (offsets, velocity)
    padded = ghosts(jnp.concatenate([position, weight[None]], axis=0))
    ghost_mass = padded[3]
    padded_pos = padded[:3]
    for step in range(SUBSTEPS):
        if step > 0:
            padded_pos = ghosts(position)
        speed = speed + 0.1 * forces(position, padded_pos, ghost_mass)
        position = position + 0.1 * speed
    return (position, speed)


def solution(mesh):
    return jax.shard_map(
        shards,
        mesh=mesh,
        in_specs=(
            P(None, "gx", "gy", "gz", None),
            P(None, "gx", "gy", "gz", None),
            P("gx", "gy", "gz", None),
            P("gx", "gy", "gz"),
        ),
        out_specs=(P(None, "gx", "gy", "gz", None), P(None, "gx", "gy", "gz", None)),
        check_vma=False,
    )
```

profile of v0, /device:TPU:51, one launch (start us, length us, event | category | flops | bytes accessed | tf_op | source)
XLA Modules:
  0.0 370.3 jit_solution(5101973556725544183)
XLA Ops:
  2.2 4.0 %collective-permute-start = (f32[4,1,4,1,256]{4,2,1,0,3:T(4,128)S(1)}, f32[4,1,4,1,256]{4,2,1,0,3:T(4,128)S(1)}, u32[]{:S(2)}, u32[]{:S(2)}) collective-permute-start(f32[4,1,4,1,256]{4,2,1,0,3:T(4,128)S(1)} %get-tuple-element.338), channel_id=1, source_target_pairs={{0,256},{256,512},{512,768},{768,0},{1,257},{257,513},{513,769},{7... | collective-permute-start | bytes 49160 | tf_op jit(solution)/shard_map/ppermute | solution.py:16
  6.2 3.3 collective-permute-start.1
  9.6 2.2 collective-permute-done.1
  11.8 4.9 %collective-permute-start.2 = (f32[4,4,1,1,256]{4,2,1,0,3:T(1,128)S(1)}, f32[4,4,1,1,256]{4,2,1,0,3:T(1,128)S(1)}, u32[]{:S(2)}, u32[]{:S(2)}) collective-permute-start(f32[4,4,1,1,256]{4,2,1,0,3:T(1,128)S(1)} %get-tuple-element.326), channel_id=1, source_target_pairs={{0,16},{16,32},{32,48},{48,64},{64,80},{80,96},{96,112},{112,128},... | collective-permute-start | bytes 49160 | tf_op jit(solution)/shard_map/ppermute | solution.py:16
  16.8 15.0 %collective-permute-start.3 = (f32[4,4,1,1,256]{4,2,1,0,3:T(1,128)S(1)}, f32[4,4,1,1,256]{4,2,1,0,3:T(1,128)S(1)}, u32[]{:S(2)}, u32[]{:S(2)}) collective-permute-start(f32[4,4,1,1,256]{4,2,1,0,3:T(1,128)S(1)} %get-tuple-element.327), channel_id=1, source_target_pairs={{16,0},{32,16},{48,32},{64,48},{80,64},{96,80},{112,96},{128,112},... | collective-permute-start | bytes 49160 | tf_op jit(solution)/shard_map/ppermute | solution.py:19
  32.7 5.0 %collective-permute-start.4 = (f32[4,4,6,1,256]{4,2,1,0,3:T(8,128)S(1)}, f32[4,4,6,1,256]{4,2,1,0,3:T(8,128)S(1)}, u32[]{:S(2)}, u32[]{:S(2)}) collective-permute-start(f32[4,4,6,1,256]{4,2,1,0,3:T(8,128)S(1)} %get-tuple-element.307), channel_id=1, source_target_pairs={{0,1},{1,2},{2,3},{3,4},{4,5},{5,6},{6,7},{7,8},{8,9},{9,10},{10,1... | collective-permute-start | bytes 294920 | tf_op jit(solution)/shard_map/ppermute | solution.py:16
  38.4 1.2 collective-permute-done.4
  39.6 3.7 collective-permute-done.5
  44.3 149.1 %while.51 = (s32[]{:T(128)}, f32[2,3,4,256]{3,2,0,1:T(4,128)S(1)}, f32[2,27,3,4,256]{4,3,0,2,1:T(4,128)S(1)}, f32[2,27,4,256]{3,2,1,0:T(4,128)S(1)}, f32[2,3,4,2...) while((s32[]{:T(128)}, f32[2,3,4,256]{3,2,0,1:T(4,128)S(1)}, ...), condition=%wide.region_5.6_spmd.clone, body=%wide.region_0.5_spmd.sunk.clone.sunk | while | flops 7605253 | bytes 5263704 | solution.py:84
  44.4 74.4 %while.54 = (s32[]{:T(128)}, f32[3,4,256]{2,1,0:T(4,128)S(1)}, f32[27,4,256]{2,1,0:T(4,128)S(1)}, f32[27,3,4,256]{3,2,1,0:T(4,128)S(1)}, f32[3,4,256]{2,1,0:T(4,...) while((s32[]{:T(128)}, f32[3,4,256]{2,1,0:T(4,128)S(1)}, ...), condition=%wide.region_4.4_spmd.clone.clone, body=%wide.region_1.3_spmd.sunk.clone.clone.sunk | while | flops 7605251 | bytes 4329627 | solution.py:81
  48.9 0.9 multiply_reduce_fusion.11
  51.7 0.9 multiply_reduce_fusion.11
  54.4 0.9 multiply_reduce_fusion.11
  57.2 0.9 multiply_reduce_fusion.11
  60.0 0.9 multiply_reduce_fusion.11
  62.7 0.9 multiply_reduce_fusion.11
  65.5 0.9 multiply_reduce_fusion.11
  73.7 0.9 multiply_reduce_fusion.11
  76.5 0.9 multiply_reduce_fusion.11
  79.3 0.9 multiply_reduce_fusion.11
  82.0 0.9 multiply_reduce_fusion.11
  84.8 0.9 multiply_reduce_fusion.11
  87.5 0.9 multiply_reduce_fusion.11
  90.3 0.9 multiply_reduce_fusion.11
  101.3 0.9 multiply_reduce_fusion.11
  104.1 0.9 multiply_reduce_fusion.11
  106.8 0.9 multiply_reduce_fusion.11
  109.6 0.9 multiply_reduce_fusion.11
  112.3 0.9 multiply_reduce_fusion.11
  115.1 0.9 multiply_reduce_fusion.11
  117.8 0.9 multiply_reduce_fusion.11
  118.9 74.4 %while.54 = (s32[]{:T(128)}, f32[3,4,256]{2,1,0:T(4,128)S(1)}, f32[27,4,256]{2,1,0:T(4,128)S(1)}, f32[27,3,4,256]{3,2,1,0:T(4,128)S(1)}, f32[3,4,256]{2,1,0:T(4,...) while((s32[]{:T(128)}, f32[3,4,256]{2,1,0:T(4,128)S(1)}, ...), condition=%wide.region_4.4_spmd.clone.clone, body=%wide.region_1.3_spmd.sunk.clone.clone.sunk | while | flops 7605251 | bytes 4329627 | solution.py:81
  120.7 0.9 multiply_reduce_fusion.11
  123.5 0.9 multiply_reduce_fusion.11
  126.2 0.9 multiply_reduce_fusion.11
  129.0 0.9 multiply_reduce_fusion.11
  131.8 0.9 multiply_reduce_fusion.11
  134.5 0.9 multiply_reduce_fusion.11
  142.8 0.9 multiply_reduce_fusion.11
  145.5 0.9 multiply_reduce_fusion.11
  148.3 0.9 multiply_reduce_fusion.11
  151.1 0.9 multiply_reduce_fusion.11
  153.8 0.9 multiply_reduce_fusion.11
  156.6 0.9 multiply_reduce_fusion.11
  159.3 0.9 multiply_reduce_fusion.11
  170.4 0.9 multiply_reduce_fusion.11
  173.1 0.9 multiply_reduce_fusion.11
  175.9 0.9 multiply_reduce_fusion.11
  178.6 0.9 multiply_reduce_fusion.11
  181.4 0.9 multiply_reduce_fusion.11
  184.1 0.9 multiply_reduce_fusion.11
  186.9 0.9 multiply_reduce_fusion.11
  193.5 5.9 %collective-permute-start.6 = (f32[3,1,4,1,256]{4,3,2,1,0:T(1,128)S(1)}, f32[3,1,4,1,256]{4,3,2,1,0:T(1,128)S(1)}, u32[]{:S(2)}, u32[]{:S(2)}) collective-permute-start(f32[3,1,4,1,256]{4,3,2,1,0:T(1,128)S(1)} %get-tuple-element.342), channel_id=1, source_target_pairs={{0,256},{256,512},{512,768},{768,0},{1,257},{257,513},{513,769},{7... | collective-permute-start | bytes 36872 | tf_op jit(solution)/shard_map/ppermute | solution.py:16
  199.4 1.9 collective-permute-start.7
  201.4 3.5 collective-permute-done.7
  204.9 1.9 collective-permute-start.8
  206.9 6.0 %collective-permute-start.9 = (f32[3,4,1,1,256]{4,3,2,1,0:T(1,128)S(1)}, f32[3,4,1,1,256]{4,3,2,1,0:T(1,128)S(1)}, u32[]{:S(2)}, u32[]{:S(2)}) collective-permute-start(f32[3,4,1,1,256]{4,3,2,1,0:T(1,128)S(1)} %get-tuple-element.337), channel_id=1, source_target_pairs={{16,0},{32,16},{48,32},{64,48},{80,64},{96,80},{112,96},{128,112},... | collective-permute-start | bytes 36872 | tf_op jit(solution)/shard_map/ppermute | solution.py:19
  213.8 2.9 collective-permute-start.10
  216.9 1.9 collective-permute-done.11
  219.0 1.0 stack.12
  220.5 149.1 %while.53 = (s32[]{:T(128)}, f32[2,3,4,256]{3,2,0,1:T(4,128)S(1)}, f32[2,27,3,4,256]{4,3,2,1,0:T(4,128)S(1)}, f32[2,27,4,256]{3,2,1,0:T(4,128)S(1)}, f32[2,3,4,2...) while((s32[]{:T(128)}, f32[2,3,4,256]{3,2,0,1:T(4,128)S(1)}, ...), condition=%wide.region_11.12_spmd.clone, body=%wide.region_6.11_spmd.sunk.clone.sunk | while | flops 7605253 | bytes 5263704 | solution.py:84
  220.6 74.4 %while.55 = (s32[]{:T(128)}, f32[3,4,256]{2,1,0:T(4,128)S(1)}, f32[27,4,256]{2,1,0:T(4,128)S(1)}, f32[27,3,4,256]{3,2,1,0:T(4,128)S(1)}, f32[3,4,256]{2,1,0:T(4,...) while((s32[]{:T(128)}, f32[3,4,256]{2,1,0:T(4,128)S(1)}, ...), condition=%wide.region_10.10_spmd.clone.clone, body=%wide.region_7.9_spmd.sunk.clone.clone.sunk | while | flops 7605251 | bytes 4329627 | solution.py:81
  222.3 0.9 multiply_reduce_fusion.9
  295.1 74.4 %while.55 = (s32[]{:T(128)}, f32[3,4,256]{2,1,0:T(4,128)S(1)}, f32[27,4,256]{2,1,0:T(4,128)S(1)}, f32[27,3,4,256]{3,2,1,0:T(4,128)S(1)}, f32[3,4,256]{2,1,0:T(4,...) while((s32[]{:T(128)}, f32[3,4,256]{2,1,0:T(4,128)S(1)}, ...), condition=%wide.region_10.10_spmd.clone.clone, body=%wide.region_7.9_spmd.sunk.clone.clone.sunk | while | flops 7605251 | bytes 4329627 | solution.py:81
  (824 shorter events, 259.1 us)
Async XLA Ops:
  2.2 7.4 %collective-permute-start = (f32[4,1,4,1,256]{4,2,1,0,3:T(4,128)S(1)}, f32[4,1,4,1,256]{4,2,1,0,3:T(4,128)S(1)}, u32[]{:S(2)}, u32[]{:S(2)}) collective-permute-start(f32[4,1,4,1,256]{4,2,1,0,3:T(4,128)S(1)} %get-tuple-element.338), channel_id=1, source_target_pairs={{0,256},{256,512},{512,768},{768,0},{1,257},{257,513},{513,769},{7... | collective-permute-start | bytes 49160 | tf_op jit(solution)/shard_map/ppermute | solution.py:16
  6.2 5.6 %collective-permute-start.1 = (f32[4,1,4,1,256]{4,2,1,0,3:T(4,128)S(1)}, f32[4,1,4,1,256]{4,2,1,0,3:T(4,128)S(1)}, u32[]{:S(2)}, u32[]{:S(2)}) collective-permute-start(f32[4,1,4,1,256]{4,2,1,0,3:T(4,128)S(1)} %get-tuple-element.339), channel_id=1, source_target_pairs={{256,0},{512,256},{768,512},{0,768},{257,1},{513,257},{769,513},{1... | collective-permute-start | bytes 49160 | tf_op jit(solution)/shard_map/ppermute | solution.py:19
  11.8 19.9 %collective-permute-start.2 = (f32[4,4,1,1,256]{4,2,1,0,3:T(1,128)S(1)}, f32[4,4,1,1,256]{4,2,1,0,3:T(1,128)S(1)}, u32[]{:S(2)}, u32[]{:S(2)}) collective-permute-start(f32[4,4,1,1,256]{4,2,1,0,3:T(1,128)S(1)} %get-tuple-element.326), channel_id=1, source_target_pairs={{0,16},{16,32},{32,48},{48,64},{64,80},{80,96},{96,112},{112,128},... | collective-permute-start | bytes 49160 | tf_op jit(solution)/shard_map/ppermute | solution.py:16
  16.7 27.2 %copy-start = (f32[3,2,4,1,256]{4,3,2,1,0:T(1,128)S(1)}, f32[3,2,4,1,256]{4,3,2,1,0:T(1,128)}, u32[]{:S(2)}) copy-start(f32[3,2,4,1,256]{4,3,2,1,0:T(1,128)} %param.14) | copy-start | bytes 73732
  16.8 15.8 %collective-permute-start.3 = (f32[4,4,1,1,256]{4,2,1,0,3:T(1,128)S(1)}, f32[4,4,1,1,256]{4,2,1,0,3:T(1,128)S(1)}, u32[]{:S(2)}, u32[]{:S(2)}) collective-permute-start(f32[4,4,1,1,256]{4,2,1,0,3:T(1,128)S(1)} %get-tuple-element.327), channel_id=1, source_target_pairs={{16,0},{32,16},{48,32},{64,48},{80,64},{96,80},{112,96},{128,112},... | collective-permute-start | bytes 49160 | tf_op jit(solution)/shard_map/ppermute | solution.py:19
  32.7 7.0 %collective-permute-start.4 = (f32[4,4,6,1,256]{4,2,1,0,3:T(8,128)S(1)}, f32[4,4,6,1,256]{4,2,1,0,3:T(8,128)S(1)}, u32[]{:S(2)}, u32[]{:S(2)}) collective-permute-start(f32[4,4,6,1,256]{4,2,1,0,3:T(8,128)S(1)} %get-tuple-element.307), channel_id=1, source_target_pairs={{0,1},{1,2},{2,3},{3,4},{4,5},{5,6},{6,7},{7,8},{8,9},{9,10},{10,1... | collective-permute-start | bytes 294920 | tf_op jit(solution)/shard_map/ppermute | solution.py:16
  37.7 5.6 %collective-permute-start.5 = (f32[4,4,6,1,256]{4,2,1,3,0:T(8,128)S(1)}, f32[4,4,6,1,256]{4,2,1,3,0:T(8,128)S(1)}, u32[]{:S(2)}, u32[]{:S(2)}) collective-permute-start(f32[4,4,6,1,256]{4,2,1,3,0:T(8,128)S(1)} %get-tuple-element.306), channel_id=1, source_target_pairs={{1,0},{2,1},{3,2},{4,3},{5,4},{6,5},{7,6},{8,7},{9,8},{10,9},{11,1... | collective-permute-start | bytes 294920 | tf_op jit(solution)/shard_map/ppermute | solution.py:19
  44.3 149.2 %copy-start.1 = (f32[3,2,4,1,256]{4,3,2,1,0:T(1,128)S(1)}, f32[3,2,4,1,256]{4,3,2,1,0:T(1,128)}, u32[]{:S(2)}) copy-start(f32[3,2,4,1,256]{4,3,2,1,0:T(1,128)} %param.15) | copy-start | bytes 73732
  193.5 7.9 %collective-permute-start.6 = (f32[3,1,4,1,256]{4,3,2,1,0:T(1,128)S(1)}, f32[3,1,4,1,256]{4,3,2,1,0:T(1,128)S(1)}, u32[]{:S(2)}, u32[]{:S(2)}) collective-permute-start(f32[3,1,4,1,256]{4,3,2,1,0:T(1,128)S(1)} %get-tuple-element.342), channel_id=1, source_target_pairs={{0,256},{256,512},{512,768},{768,0},{1,257},{257,513},{513,769},{7... | collective-permute-start | bytes 36872 | tf_op jit(solution)/shard_map/ppermute | solution.py:16
  199.4 5.5 %collective-permute-start.7 = (f32[3,1,4,1,256]{4,3,2,1,0:T(1,128)S(1)}, f32[3,1,4,1,256]{4,3,2,1,0:T(1,128)S(1)}, u32[]{:S(2)}, u32[]{:S(2)}) collective-permute-start(f32[3,1,4,1,256]{4,3,2,1,0:T(1,128)S(1)} %get-tuple-element.343), channel_id=1, source_target_pairs={{256,0},{512,256},{768,512},{0,768},{257,1},{513,257},{769,513},{1... | collective-permute-start | bytes 36872 | tf_op jit(solution)/shard_map/ppermute | solution.py:19
  204.9 8.0 %collective-permute-start.8 = (f32[3,4,1,1,256]{4,3,2,1,0:T(1,128)S(1)}, f32[3,4,1,1,256]{4,3,2,1,0:T(1,128)S(1)}, u32[]{:S(2)}, u32[]{:S(2)}) collective-permute-start(f32[3,4,1,1,256]{4,3,2,1,0:T(1,128)S(1)} %get-tuple-element.336), channel_id=1, source_target_pairs={{0,16},{16,32},{32,48},{48,64},{64,80},{80,96},{96,112},{112,128},... | collective-permute-start | bytes 36872 | tf_op jit(solution)/shard_map/ppermute | solution.py:16
  206.9 6.8 %collective-permute-start.9 = (f32[3,4,1,1,256]{4,3,2,1,0:T(1,128)S(1)}, f32[3,4,1,1,256]{4,3,2,1,0:T(1,128)S(1)}, u32[]{:S(2)}, u32[]{:S(2)}) collective-permute-start(f32[3,4,1,1,256]{4,3,2,1,0:T(1,128)S(1)} %get-tuple-element.337), channel_id=1, source_target_pairs={{16,0},{32,16},{48,32},{64,48},{80,64},{96,80},{112,96},{128,112},... | collective-permute-start | bytes 36872 | tf_op jit(solution)/shard_map/ppermute | solution.py:19
  213.7 5.0 %collective-permute-start.11 = (f32[3,4,6,1,256]{4,3,2,1,0:T(1,128)S(1)}, f32[3,4,6,1,256]{4,3,2,1,0:T(1,128)S(1)}, u32[]{:S(2)}, u32[]{:S(2)}) collective-permute-start(f32[3,4,6,1,256]{4,3,2,1,0:T(1,128)S(1)} %pad_maximum_fusion.3), channel_id=1, source_target_pairs={{1,0},{2,1},{3,2},{4,3},{5,4},{6,5},{7,6},{8,7},{9,8},{10,9},{11,1... | collective-permute-start | bytes 221192 | tf_op jit(solution)/shard_map/ppermute | solution.py:19
  213.8 5.1 %collective-permute-start.10 = (f32[3,4,6,1,256]{4,3,2,1,0:T(1,128)S(1)}, f32[3,4,6,1,256]{4,3,2,1,0:T(1,128)S(1)}, u32[]{:S(2)}, u32[]{:S(2)}) collective-permute-start(f32[3,4,6,1,256]{4,3,2,1,0:T(1,128)S(1)} %pad_maximum_fusion.3), channel_id=1, source_target_pairs={{0,1},{1,2},{2,3},{3,4},{4,5},{5,6},{6,7},{7,8},{8,9},{9,10},{10,1... | collective-permute-start | bytes 221192 | tf_op jit(solution)/shard_map/ppermute | solution.py:16
where the time goes:
time: 374 us; the launch traced here: 370 us
  other arithmetic  217 us (58%)
  local copies, waits for them, and re-layouts  81.5 us (22%)
  starting transfers between devices  51 us (14%)
  waiting for transfers between devices  14.1 us (4%)
  loops' own time  5.74 us (2%)
    reduce_sum x108, other arithmetic, pair_tile(): return jnp.sum(scaled[None] * dist, axis=-1)  102 us
    add x108, local copies, waits for them, and re-layouts, pair_tile(): dist = dist + shift.reshape((3,) + (1,) * (dist.ndim - 1))  75.5 us
    mul x108, other arithmetic, pair_tile(): scaled = source_mass[..., None, :] * factor  59.1 us
    reduce_sum x108, other arithmetic, pair_tile(): square = jnp.sum(dist * dist, axis=0)  51.7 us
    ppermute x6, starting transfers between devices, with_halo(): lax.ppermute(lax.slice_in_dim(block, 0, width, axis=dim), axis, backward)  26.3 us
    ppermute x6, starting transfers between devices, with_halo(): lax.ppermute(lax.slice_in_dim(block, block.shape[dim] - width, None, axis...  24.8 us
    ppermute x6, waiting for transfers between devices, with_halo(): lax.ppermute(lax.slice_in_dim(block, 0, width, axis=dim), axis, backward)  12.8 us
  transfers between devices with their start and end apart: 12, of which 7 were waited for; matrix products, arithmetic and copies ran while one was open for 0% of the time, Pallas kernels for 0%

commit v1 on v0

v1 whole, which is shorter than its diff:
```python
import functools
import jax
import jax.numpy as jnp
from jax import lax
from jax.experimental import pallas as pl
from jax.experimental.pallas import tpu as pltpu
from jax.sharding import PartitionSpec as P

SUBSTEPS = 2

RUN = 40
U = 4
MOST = 10
FEAT = 4


def split3(x):
    h = x.astype(jnp.bfloat16).astype(jnp.float32)
    rest = x - h
    m = rest.astype(jnp.bfloat16).astype(jnp.float32)
    low = (rest - m).astype(jnp.bfloat16).astype(jnp.float32)
    return h, m, low


def force_kernel(dims, counts_ref, src_ref, vel_ref, pos_out, vel_out,
                 table, feat, coef, tgt, acc, stage_a, stage_b, bounds, items):
    nx, ny, nz = dims
    ex, ey, ez = nx + 2, ny + 2, nz + 2
    row = lax.broadcasted_iota(jnp.int32, (8, 128), 0)
    lane = lax.broadcasted_iota(jnp.int32, (8, 128), 1)
    comp = row % 4
    center = (nx / 2.0, ny / 2.0, nz / 2.0)

    def frame(x, y, z):
        shift = [c - m - 1.0 for c, m in zip((x, y, z), center)]
        return jnp.where(comp == 0, shift[0], jnp.where(comp == 1, shift[1], jnp.where(comp == 2, shift[2], 0.0)))

    table[...] = jnp.zeros_like(table)
    ends = []
    points = {}
    for x in range(ex):
        off = jnp.int32(x * RUN * 128)
        for y in range(ey):
            points[(x, y)] = off
            for z in range(ez):
                e = (x * ey + y) * ez + z
                tile = src_ref[e] + frame(x, y, z)
                s = off & 127
                base = lax.shift_right_logical(off, 7)
                low = pltpu.roll(tile, s, 1)
                high = pltpu.roll(low, 4, 0)
                keep = lane < s
                table[base] = jnp.where(keep, table[base], low)
                table[base + 1] = jnp.where(keep, low, high)
                table[base + 2] = jnp.where(keep, high, 0.0)
                off = off + counts_ref[e]
        points[(x, ey)] = off
        ends.append(off)

    n = jnp.int32(0)
    for x in range(nx):
        for y in range(ny):
            for r in range(3):
                start = points[(x + r, y)]
                end = points[(x + r, y + 3)]
                first = lax.shift_right_logical(start, 7)
                last = lax.shift_right_logical(end + 127, 7)
                chunks = lax.shift_right_logical(last - first + 1, 1)
                tag = ((x * ny + y) * 4 + r)
                bounds[0, tag] = start
                bounds[1, tag] = end
                for j in range(MOST):
                    items[n + j] = first + (2 * j + tag * 256)
                n = n + chunks
    for j in range(4 * U):
        items[n + j] = (nx * ny * 4 - 1) * 256
    bounds[0, nx * ny * 4 - 1] = 0
    bounds[1, nx * ny * 4 - 1] = 0

    def norm(v):
        sq = jnp.where(row < 3, v * v, 0.0)
        sq = sq + pltpu.roll(sq, 4, 0)
        sq = sq + pltpu.roll(sq, 2, 0)
        return sq + pltpu.roll(sq, 1, 0)

    zeros = jnp.zeros((8, 128), jnp.float32)

    def features(t):
        v = table[t]
        full = jnp.where(row < 3, v, jnp.where(row < 6, pltpu.roll(v * v, 3, 0), jnp.where(row == 6, 1.0, 0.0)))
        h, m, low = split3(full)
        feat[t] = jnp.concatenate([h, m, low, h, m, h], axis=0).astype(jnp.bfloat16)
        mass = jnp.broadcast_to(v[3:4], (8, 128))
        gh, gm, gl = split3(jnp.where(row < 3, v, 1.0) * mass)
        coef[t] = jnp.concatenate([gh, gm, gl, zeros], axis=0)

    for x in range(ex):
        first = x * RUN
        count = lax.shift_right_logical(ends[x] + 127, 7) - first + 1

        def group(k, c, first=first):
            for j in range(FEAT):
                features(first + FEAT * k + j)
            return c

        lax.fori_loop(0, (count + FEAT - 1) // FEAT, group, 0)

    for x in range(nx):
        for y in range(ny):
            e = ((x + 1) * ey + y + 1) * ez + 1
            tile = src_ref[e] + frame(x + 1, y + 1, 1)
            for half in range(2):
                v = tile if half == 0 else pltpu.roll(tile, 4, 0)
                full = jnp.where(row < 3, -2.0 * v, jnp.where(row < 6, 1.0, jnp.where(row == 6, norm(v) + 0.01, 0.0)))
                h, m, low = split3(full)
                stacked = jnp.concatenate([h, h, h, m, m, low], axis=0)
                tgt[x * ny + y, :, half * 128:(half + 1) * 128] = stacked.astype(jnp.bfloat16)
    acc[...] = jnp.zeros_like(acc)

    lane32 = lax.broadcasted_iota(jnp.int32, (32, 256), 1)

    def squares(k, u, stage):
        code = items[k]
        t = code & 255
        leaf = lax.shift_right_logical(code, 10)
        f = jnp.concatenate([feat[t], feat[t + 1]], axis=1)
        stage[u] = lax.dot_general(f, tgt[leaf], (((0,), (0,)), ((), ())), preferred_element_type=jnp.float32)

    def gather(k, u, stage):
        code = items[k]
        t = code & 255
        tag = lax.shift_right_logical(code, 8)
        leaf = lax.shift_right_logical(code, 10)
        lo = bounds[0, tag] - t * 128
        hi = bounds[1, tag] - t * 128
        q = stage[u]
        r = lax.rsqrt(q)
        a = r * jnp.maximum(1.01 - q, 0.0)
        w = a * a * r
        whi = w.astype(jnp.bfloat16)
        wlo = (w - whi.astype(jnp.float32)).astype(jnp.bfloat16)
        cc = jnp.concatenate([coef[t], coef[t + 1]], axis=1)
        cc = jnp.where((lane32 >= lo) & (lane32 < hi), cc, 0.0).astype(jnp.bfloat16)
        out = jnp.dot(cc, whi, preferred_element_type=jnp.float32)
        out = out + jnp.dot(cc, wlo, preferred_element_type=jnp.float32)
        acc[leaf] = acc[leaf] + out

    for u in range(U):
        squares(u, u, stage_a)

    def step(i, c):
        k = i * (2 * U)
        for u in range(U):
            squares(k + U + u, u, stage_b)
            gather(k + u, u, stage_a)
        for u in range(U):
            squares(k + 2 * U + u, u, stage_a)
            gather(k + U + u, u, stage_b)
        return c

    lax.fori_loop(0, (n + 2 * U - 1) // (2 * U), step, 0)

    for x in range(nx):
        for y in range(ny):
            leaf = x * ny + y
            e = ((x + 1) * ey + y + 1) * ez + 1
            total = acc[leaf]
            total = total[0:8] + total[8:16] + total[16:24]
            tile = src_ref[e]
            where = tile + frame(x + 1, y + 1, 1)
            parts = []
            for half in range(2):
                v = where if half == 0 else pltpu.roll(where, 4, 0)
                part = total[:, half * 128:(half + 1) * 128]
                parts.append(part - v * jnp.broadcast_to(part[3:4], (8, 128)))
            kick = jnp.where(row < 4, parts[0], pltpu.roll(parts[1], 4, 0))
            kick = jnp.where(comp < 3, kick, 0.0)
            speed = vel_ref[leaf] + 0.1 * kick
            vel_out[leaf] = speed
            pos_out[leaf] = tile + 0.1 * speed


def forces(counts, source, velocity, dims):
    nx, ny, nz = dims
    ex, ey, ez = nx + 2, ny + 2, nz + 2
    leaves = nx * ny
    tiles = ex * RUN
    shape = jax.ShapeDtypeStruct((leaves, 8, 128), jnp.float32)
    return pl.pallas_call(
        functools.partial(force_kernel, dims),
        out_shape=(shape, shape),
        in_specs=[pl.BlockSpec(memory_space=pltpu.SMEM), pl.BlockSpec(memory_space=pltpu.VMEM),
                  pl.BlockSpec(memory_space=pltpu.VMEM)],
        out_specs=(pl.BlockSpec(memory_space=pltpu.VMEM), pl.BlockSpec(memory_space=pltpu.VMEM)),
        scratch_shapes=[
            pltpu.VMEM((tiles, 8, 128), jnp.float32),
            pltpu.VMEM((tiles, 48, 128), jnp.bfloat16),
            pltpu.VMEM((tiles, 32, 128), jnp.float32),
            pltpu.VMEM((leaves, 48, 256), jnp.bfloat16),
            pltpu.VMEM((leaves, 32, 256), jnp.float32),
            pltpu.VMEM((U, 256, 256), jnp.float32),
            pltpu.VMEM((U, 256, 256), jnp.float32),
            pltpu.SMEM((2, leaves * 4), jnp.int32),
            pltpu.SMEM((leaves * 3 * MOST + 4 * U,), jnp.int32),
        ],
        name="forces",
    )(counts, source, velocity)

OFFSETS = sorted(
    [(a, b, c) for a in (-1, 0, 1) for b in (-1, 0, 1) for c in (-1, 0, 1) if (a, b, c) != (0, 0, 0)],
    key=lambda o: (-abs(o[0]), -abs(o[1]), -abs(o[2]), o),
)
AXES = ("gx", "gy", "gz")


def exchange_kernel(sizes, dims, own_ref, ext_ref, local_sem, send_sem, recv_sem):
    me = [lax.axis_index(axis) for axis in AXES]
    peers = [tuple(lax.rem(m + o + n, n) for m, o, n in zip(me, offset, sizes)) for offset in OFFSETS]
    barrier = pltpu.get_barrier_semaphore()
    for peer in peers:
        pl.semaphore_signal(barrier, inc=1, device_id=peer, device_id_type=pl.DeviceIdType.MESH)
    middle = pltpu.make_async_copy(own_ref, ext_ref.at[tuple(pl.ds(1, d) for d in dims)], local_sem)
    middle.start()
    pl.semaphore_wait(barrier, len(peers))
    copies = []
    for k, (offset, peer) in enumerate(zip(OFFSETS, peers)):
        source = tuple(pl.ds(0, d) if o == 0 else pl.ds(d - 1 if o > 0 else 0, 1) for o, d in zip(offset, dims))
        target = tuple(pl.ds(1, d) if o == 0 else pl.ds(0 if o > 0 else d + 1, 1) for o, d in zip(offset, dims))
        copy = pltpu.make_async_remote_copy(
            src_ref=own_ref.at[source],
            dst_ref=ext_ref.at[target],
            send_sem=send_sem.at[k],
            recv_sem=recv_sem.at[k],
            device_id=peer,
            device_id_type=pl.DeviceIdType.MESH,
        )
        copy.start()
        copies.append(copy)
    middle.wait()
    for copy in copies:
        copy.wait()


def exchange(own, sizes, collective_id):
    dims = own.shape[:3]
    count = len(OFFSETS)
    return pl.pallas_call(
        functools.partial(exchange_kernel, sizes, dims),
        out_shape=jax.ShapeDtypeStruct(tuple(d + 2 for d in dims) + (8, 128), jnp.float32),
        in_specs=[pl.BlockSpec(memory_space=pltpu.VMEM)],
        out_specs=pl.BlockSpec(memory_space=pltpu.VMEM),
        scratch_shapes=[
            pltpu.SemaphoreType.DMA,
            pltpu.SemaphoreType.DMA((count,)),
            pltpu.SemaphoreType.DMA((count,)),
        ],
        compiler_params=pltpu.CompilerParams(collective_id=collective_id, has_side_effects=True),
        name="exchange",
    )(own)


def pack(fields):
    comps, nx, ny, nz, slots = fields.shape
    split = fields.reshape(comps, nx, ny, nz, 2, slots // 2)
    return jnp.transpose(split, (1, 2, 3, 4, 0, 5)).reshape(nx, ny, nz, 8, 128)


def unpack(tiles, dims):
    nx, ny, nz = dims
    split = tiles.reshape(nx, ny, nz, 2, 4, 128)[..., :3, :]
    return jnp.transpose(split, (4, 0, 1, 2, 3, 5)).reshape(3, nx, ny, nz, 256)


def shards(sizes, offsets, velocity, mass, counts):
    dims = mass.shape[:3]
    nx, ny, nz = dims
    slot = jnp.arange(mass.shape[-1], dtype=jnp.int32)
    weight = jnp.where(slot < counts[..., None], mass, jnp.float32(0.0))
    position = pack(jnp.concatenate([offsets, weight[None]], axis=0))
    speed = pack(jnp.concatenate([velocity, jnp.zeros_like(weight)[None]], axis=0))
    speed = speed.reshape(nx * ny * nz, 8, 128)
    live = None
    for _ in range(SUBSTEPS):
        source = exchange(position, sizes, 1).reshape(-1, 8, 128)
        if live is None:
            masses = jnp.concatenate([source[:, 3], source[:, 7]], axis=1)
            live = jnp.sum((masses > 0).astype(jnp.int32), axis=1)
        position, speed = forces(live, source, speed, dims)
        position = position.reshape(nx, ny, nz, 8, 128)
    return unpack(position, dims), unpack(speed, dims)


def solution(mesh):
    vector = P(None, "gx", "gy", "gz", None)
    return jax.shard_map(
        functools.partial(shards, tuple(mesh.shape[axis] for axis in AXES)),
        mesh=mesh,
        in_specs=(vector, vector, P("gx", "gy", "gz", None), P("gx", "gy", "gz")),
        out_specs=(vector, vector),
        check_vma=False,
    )
```

time: 374 us -> 92.8 us (0.25)
  the two profiles are of different devices: /device:TPU:51 before, /device:TPU:2 now
where the time goes in v1:
time: 92.8 us; the launch traced here: 91.3 us
  Pallas kernels  83.9 us (90%)
  local copies, waits for them, and re-layouts  5.44 us (6%)
  other arithmetic  1.33 us (1%)
    pallas_call x2, Pallas kernels, exchange(): pl.pallas_call(functools.partial(exchange_kernel, sizes, dims), out_shape...  43.4 us
    pallas_call x2, Pallas kernels, forces(): pl.pallas_call(functools.partial(force_kernel, dims), out_shape=(shape, s...  40.4 us
    transpose x4, local copies, waits for them, and re-layouts, unpack(): return jnp.transpose(split, (4, 0, 1, 2, 3, 5)).reshape(3, nx, ny, nz, 256)  2.01 us

profile of v1, /device:TPU:2, one launch (start us, length us, event | category | flops | bytes accessed | tf_op | source)
XLA Modules:
  0.0 91.3 jit_solution(8887134990693891193)
XLA Ops:
  0.6 0.0 copy-start.2
  0.6 0.8 copy.6
  1.4 0.0 copy-start.3
  1.4 0.0 copy-done.2
  1.4 0.7 copy-done.3
  2.1 0.1 fusion
  2.2 0.6 pad_maximum_fusion
  2.8 29.8 %exchange.2 = f32[4,6,3,8,128]{4,3,2,1,0:T(8,128)} custom-call(f32[2,4,1,8,128]{4,3,2,1,0:T(8,128)} %bitcast.34), custom_call_target="tpu_custom_call" | custom-call | tf_op jit(solution)/shard_map/exchange/pallas_call | solution.py:247
  32.6 1.1 %fusion.1 = (f32[72,1,128]{2,1,0:T(1,128)S(1)}, f32[72,1,128]{2,1,0:T(1,128)S(1)}) fusion(f32[72,8,128]{2,1,0:T(8,128)} %bitcast.28), kind=kLoop, calls=%fused_computation.7 | loop fusion | bytes 147456 | tf_op jit(solution)/shard_map/slice | solution.py:286
  33.7 0.0 copy-start.1
  33.7 0.6 convert_reduce_fusion.counts_ref
  34.4 0.1 copy-done.1
  34.5 0.6 copy.9
  35.1 20.2 %forces.2 = (f32[8,8,128]{2,1,0:T(8,128)}, f32[8,8,128]{2,1,0:T(8,128)}) custom-call(s32[72]{0:T(128)} %convert_reduce_fusion.counts_ref, f32[72,8,128]{2,1,0:T(8,128)} %bitcast.29, f32[8,8,128]{2,1,0:T(8,128)} %bitcast.33), custom_call_target="tpu_custom_call" | custom-call | tf_op jit(solution)/shard_map/forces/pallas_call | solution.py:189
  55.3 13.6 %exchange.3 = f32[4,6,3,8,128]{4,3,2,1,0:T(8,128)} custom-call(f32[2,4,1,8,128]{4,3,2,1,0:T(8,128)} %bitcast.36), custom_call_target="tpu_custom_call" | custom-call | tf_op jit(solution)/shard_map/exchange/pallas_call | solution.py:247
  69.0 20.2 %forces.3 = (f32[8,8,128]{2,1,0:T(8,128)}, f32[8,8,128]{2,1,0:T(8,128)}) custom-call(s32[72]{0:T(128)} %convert_reduce_fusion.counts_ref, f32[72,8,128]{2,1,0:T(8,128)} %bitcast.30, f32[8,8,128]{2,1,0:T(8,128)} %get-tuple-element.7.vel_ref), custom_call_target="tpu_custom_call" | custom-call | tf_op jit(solution)/shard_map/forces/pallas_call | solution.py:189
  89.2 0.8 slice_bitcast_fusion.1
  89.9 0.0 copy-start
  89.9 0.6 copy.10
  90.6 0.1 copy-done
  90.7 0.6 copy.11
  (2 shorter events, 0.0 us)
Async XLA Ops:
  0.6 0.8 copy-start.2
  1.4 0.7 copy-start.3
  33.7 0.7 copy-start.1
  89.9 0.8 copy-start
